TPU v7x, 256 devices: a 8x8x2 block of a 8x8x16 slice. The times are simulated.
256 devices in a mesh: groups: 2 (over z), grid: 16 (over y, core), orb: 8 (over x).
Axes of the slice: x: 8, y: 8, z: 2, core: 2. Of those that a mesh axis runs over, the one named last changes fastest.
The devices are a block of a 8x8x16 slice.
Arguments:
- orbitals: float32 [64, 2, 128, 128, 128], P(('groups', 'orb'), None, 'grid'), parts along dimension 0, may hold values from -6 to 6
- v_local: float32 [256, 128, 128], P(('groups', 'grid')), parts along dimension 0, may hold values from -24 to 24
- occupations: float32 [64], P('groups'), parts along dimension 0, may hold values from 0.05 to 0.5
Outputs:
- orbitals_next: float32 [64, 2, 128, 128, 128], P(('groups', 'orb'), None, 'grid'), parts along dimension 0
There are 2 independent parts, one for each index of `groups`. A program takes and returns all parts, laid end to end along the dimension named above; each array names one. Nothing has to cross between parts.
All inputs are finite; a program needn't handle non-finite values.
Results may differ from a plain program's by a relative error of at most 0.00035.
Values sent between devices are 32-bit elements; how exact they have to be, the bound alone decides.
A program may use at most 64 MiB of HBM per device.

v0:
```python
import functools
import math

import jax
import jax.numpy as jnp
import numpy as np
from jax import lax
from jax.experimental import pallas as pl
from jax.experimental.pallas import tpu as pltpu
from jax.sharding import PartitionSpec as P

TIME_STEP = 0.05
KINETIC_RATE = 0.1
HARTREE_SCALE = math.pi
HIGHEST = lax.Precision.HIGHEST
MESH = pl.DeviceIdType.MESH


def wave_squared(length):
    mode_ids = np.arange(length)
    signed = np.where(mode_ids < (length + 1) // 2, mode_ids, mode_ids - length)
    return (2.0 * math.pi * signed / length) ** 2


def kinetic_table(length):
    phase = np.exp(-1j * KINETIC_RATE * wave_squared(length))
    circulant = np.fft.ifft(phase)
    ids = np.arange(length)
    full = circulant[(ids[:, None] - ids[None, :]) % length]
    return np.block([[full.real, -full.imag], [full.imag, full.real]]).astype(np.float32)


def hartley_table(length):
    ids = np.arange(length)
    angle = 2.0 * math.pi * (ids[:, None] * ids[None, :] % length) / length
    return ((np.cos(angle) + np.sin(angle)) / math.sqrt(length)).astype(np.float32)


def dot(left, right):
    return jnp.dot(left, right, precision=HIGHEST, preferred_element_type=jnp.float32)


def swap(block):
    return jnp.transpose(block, (1, 0, 2))


def kernel(
    grid_count,
    orb_count,
    occ_ref,
    psi_ref,
    left_x,
    left_y,
    right_z,
    hart_x,
    hart_y,
    hart_z,
    sq_y,
    sq_z,
    evolved_ref,
    hartree_ref,
    own,
    lines_y,
    send_a,
    recv_a,
    lines_x,
    send_b,
    density,
    parts,
    modes,
    modes_in,
    tiles,
    pencil,
    pencil_out,
    tiles_in,
    tiles_out,
    plane_in,
    plane,
    slabs,
    load_sem,
    recv_sem,
    recv_b_sem,
    send_sem,
    hart_send,
    hart_recv,
):
    g = lax.axis_index("grid")
    o = lax.axis_index("orb")
    layers, _, planes, count_y, count_z = own.shape
    count_x = planes * grid_count
    block_y = count_y // grid_count
    block_k = count_x // orb_count

    def load(l):
        return pltpu.make_async_copy(psi_ref.at[l], own.at[l], load_sem.at[l])

    for l in range(layers):
        load(l).start()

    barrier = pltpu.get_barrier_semaphore()

    def greet(axis, me, count):
        def one(off, carry):
            pl.semaphore_signal(
                barrier, inc=1, device_id={axis: lax.rem(me + off, count)}, device_id_type=MESH
            )
            return carry

        lax.fori_loop(1, count, one, 0)

    greet("grid", g, grid_count)
    greet("orb", o, orb_count)

    def send_all(axis, me, count, src, dst, s_sem, r_sem):
        def one(off, carry):
            to = lax.rem(me + off, count)
            pltpu.make_async_remote_copy(
                src_ref=src(to),
                dst_ref=dst,
                send_sem=s_sem,
                recv_sem=r_sem,
                device_id={axis: to},
                device_id_type=MESH,
            ).start()
            return carry

        lax.fori_loop(1, count, one, 0)

    def wait_for(ref, sem):
        pltpu.make_async_copy(ref, ref, sem).wait()

    def rows(start, size):
        return pl.ds(pl.multiple_of(start, 8), size)

    def along_y(l):
        load(l).wait()

        def pair(i, carry):
            both = [
                jnp.concatenate([own[l, 0, 2 * i + k], own[l, 1, 2 * i + k]], axis=0) for k in (0, 1)
            ]
            out = dot(left_y[...], jnp.concatenate(both, axis=1))
            lines_y[2 * i] = out[:, :count_z]
            lines_y[2 * i + 1] = out[:, count_z:]
            return carry

        lax.fori_loop(0, planes // 2, pair, 0)

    quads = 4 if grid_count % 4 == 0 else 1
    chunk_y = count_y // quads

    def along_z(l):
        def quad(i, carry):
            start = lax.rem(g // (grid_count // quads) + i, quads) * chunk_y
            sides = []
            for c in (0, 1):
                block = lines_y[:, rows(c * count_y + start, chunk_y), :]
                sides.append(swap(block).reshape(chunk_y * planes, count_z))
            out = dot(jnp.concatenate(sides, axis=1), right_z[...])
            for c in (0, 1):
                part = out[:, c * count_z : (c + 1) * count_z]
                send_a[l, pl.ds(start, chunk_y), c] = part.reshape(chunk_y, planes, count_z)
            return carry

        lax.fori_loop(0, quads, quad, 0)

    def forward(l):
        along_y(l)
        along_z(l)

    def launch_forward(l):
        def src(to):
            return send_a.at[l, pl.ds(to * block_y, block_y)]

        dst = recv_a.at[l, :, :, rows(g * planes, planes), :]
        pltpu.make_async_copy(src(g), dst, recv_sem.at[l]).start()
        send_all("grid", g, grid_count, src, dst, send_sem.at[0], recv_sem.at[l])

    def across_x(l):
        wait_for(recv_a.at[l], recv_sem.at[l])
        weight = occ_ref[o * layers + l]

        def pair(i, carry):
            both = [recv_a[l, 2 * i + k].reshape(2 * count_x, count_z) for k in (0, 1)]
            out = dot(left_x[...], jnp.concatenate(both, axis=1))
            for k in (0, 1):
                part = out[:, k * count_z : (k + 1) * count_z]
                lines_x[2 * i + k] = part
                squares = part[:count_x] * part[:count_x] + part[count_x:] * part[count_x:]
                if l == 0:
                    density[2 * i + k] = weight * squares
                else:
                    density[2 * i + k] += weight * squares
            return carry

        lax.fori_loop(0, block_y // 2, pair, 0)

        def turn(i, carry):
            for c in (0, 1):
                block = lines_x[:, rows(c * count_x + i * planes, planes), :]
                send_b[l, c, rows(i * planes, planes)] = swap(block)
            return carry

        lax.fori_loop(0, grid_count, turn, 0)

    def launch_back(l):
        def src(to):
            return send_b.at[l, :, pl.ds(to * planes, planes)]

        dst = evolved_ref.at[l, :, :, rows(g * block_y, block_y), :]
        pltpu.make_async_copy(src(g), dst, recv_b_sem).start()
        send_all("grid", g, grid_count, src, dst, send_sem.at[1], recv_b_sem)

    forward(0)
    pl.semaphore_wait(barrier, grid_count - 1 + orb_count - 1)
    launch_forward(0)
    for l in range(1, layers):
        forward(l)
        launch_forward(l)
    across_x(0)
    launch_back(0)
    for l in range(1, layers):
        across_x(l)

    send_all("orb", o, orb_count, lambda to: density.at[to], parts.at[o], hart_send.at[0], hart_recv.at[0])
    parts[o] = jnp.zeros((count_x, count_z), jnp.float32)
    wait_for(parts.at[pl.ds(0, orb_count - 1)], hart_recv.at[0])
    total = density[o]
    for k in range(orb_count):
        total += parts[k]
    modes[...] = dot(dot(hart_x[...], total), hart_z[...])

    send_all(
        "orb", o, orb_count, lambda to: modes.at[rows(to * block_k, block_k)], modes_in.at[o], hart_send.at[1], hart_recv.at[1]
    )
    modes_in[o] = modes[rows(o * block_k, block_k)]
    wait_for(modes_in.at[pl.ds(0, orb_count - 1)], hart_recv.at[1])
    tiles[...] = swap(modes_in[...])

    send_all(
        "grid", g, grid_count, lambda to: tiles.at[to], pencil.at[rows(g * block_y, block_y)], hart_send.at[2], hart_recv.at[2]
    )
    pencil[rows(g * block_y, block_y)] = tiles[g]
    if layers > 1:
        launch_back(1)
    wait_for(pencil.at[pl.ds(0, count_y - block_y)], hart_recv.at[2])

    mode_x = o * block_k + g
    signed_x = jnp.where(mode_x < (count_x + 1) // 2, mode_x, mode_x - count_x).astype(jnp.float32)
    wave_x = signed_x * (2.0 * math.pi / count_x)
    waves = wave_x * wave_x + sq_y[...] + sq_z[...]
    anchor = waves <= 0.0
    scale = jnp.where(anchor, 0.0, HARTREE_SCALE / jnp.where(anchor, 1.0, waves))
    pencil_out[...] = dot(hart_y[...], dot(hart_y[...], pencil[...]) * scale)

    send_all(
        "grid", g, grid_count, lambda to: pencil_out.at[rows(to * block_y, block_y)], tiles_in.at[g], hart_send.at[3], hart_recv.at[3]
    )
    tiles_in[g] = pencil_out[rows(g * block_y, block_y)]
    if layers > 2:
        launch_back(2)
    wait_for(tiles_in.at[pl.ds(0, grid_count - 1)], hart_recv.at[3])
    tiles_out[...] = swap(tiles_in[...])

    send_all(
        "orb", o, orb_count, lambda to: tiles_out.at[to], plane_in.at[rows(o * block_k, block_k)], hart_send.at[4], hart_recv.at[4]
    )
    plane_in[rows(o * block_k, block_k)] = tiles_out[o]
    wait_for(plane_in.at[pl.ds(0, count_x - block_k)], hart_recv.at[4])
    plane[...] = dot(dot(hart_x[...], plane_in[...]), hart_z[...])

    mine = slabs.at[o]
    send_all(
        "grid", g, grid_count, lambda to: plane.at[rows(to * planes, planes)], slabs.at[o, g], hart_send.at[5], hart_recv.at[5]
    )
    slabs[o, g] = plane[rows(g * planes, planes)]
    for l in range(3, layers):
        launch_back(l)
    wait_for(mine.at[pl.ds(0, grid_count - 1)], hart_recv.at[5])

    send_all("orb", o, orb_count, lambda to: slabs.at[o], slabs.at[o], hart_send.at[6], hart_recv.at[6])
    wait_for(slabs.at[pl.ds(0, orb_count - 1)], hart_recv.at[6])

    def spread(i, carry):
        hartree_ref[:, rows(i * block_y, block_y), :] = swap(slabs[:, i])
        return carry

    lax.fori_loop(0, grid_count, spread, 0)

    wait_for(evolved_ref, recv_b_sem)
    sent_a = send_a.at[:, pl.ds(0, count_y - block_y)]
    wait_for(sent_a, send_sem.at[0])
    sent_b = send_b.at[:, :, pl.ds(0, count_x - planes)]
    wait_for(sent_b, send_sem.at[1])
    wait_for(density.at[pl.ds(0, orb_count - 1)], hart_send.at[0])
    wait_for(modes.at[pl.ds(0, count_x - block_k)], hart_send.at[1])
    wait_for(tiles.at[pl.ds(0, grid_count - 1)], hart_send.at[2])
    wait_for(pencil_out.at[pl.ds(0, count_y - block_y)], hart_send.at[3])
    wait_for(tiles_out.at[pl.ds(0, orb_count - 1)], hart_send.at[4])
    wait_for(plane.at[pl.ds(0, count_x - planes)], hart_send.at[5])
    wait_for(slabs.at[pl.ds(0, orb_count - 1)], hart_send.at[6])


def body(grid_count, orb_count, orbitals, v_local, occupations):
    layers, _, planes, count_y, count_z = orbitals.shape
    count_x = planes * grid_count
    block_y = count_y // grid_count
    block_k = count_x // orb_count
    assert block_y == orb_count and block_k == grid_count

    f32 = jnp.float32
    tables = (
        kinetic_table(count_x),
        kinetic_table(count_y),
        kinetic_table(count_z).T,
        hartley_table(count_x),
        hartley_table(count_y),
        hartley_table(count_z),
        wave_squared(count_y).astype(np.float32)[:, None],
        wave_squared(count_z).astype(np.float32)[None, :],
    )
    shared = {}
    tables = [shared.setdefault((t.shape, t.tobytes()), jnp.asarray(t)) for t in tables]
    vmem = pl.BlockSpec(memory_space=pltpu.VMEM)
    anyspace = pl.BlockSpec(memory_space=pl.ANY)
    evolved, hartree = pl.pallas_call(
        functools.partial(kernel, grid_count, orb_count),
        out_shape=(
            jax.ShapeDtypeStruct(orbitals.shape, f32),
            jax.ShapeDtypeStruct((planes, count_y, count_z), f32),
        ),
        in_specs=[pl.BlockSpec(memory_space=pltpu.SMEM), anyspace] + [vmem] * 8,
        out_specs=(anyspace, vmem),
        scratch_shapes=[
            pltpu.VMEM(orbitals.shape, f32),
            pltpu.VMEM((planes, 2 * count_y, count_z), f32),
            pltpu.VMEM((layers, count_y, 2, planes, count_z), f32),
            pltpu.VMEM((layers, block_y, 2, count_x, count_z), f32),
            pltpu.VMEM((block_y, 2 * count_x, count_z), f32),
            pltpu.VMEM((layers, 2, count_x, block_y, count_z), f32),
            pltpu.VMEM((block_y, count_x, count_z), f32),
            pltpu.VMEM((orb_count, count_x, count_z), f32),
            pltpu.VMEM((count_x, count_z), f32),
            pltpu.VMEM((orb_count, block_k, count_z), f32),
            pltpu.VMEM((grid_count, block_y, count_z), f32),
            pltpu.VMEM((count_y, count_z), f32),
            pltpu.VMEM((count_y, count_z), f32),
            pltpu.VMEM((grid_count, block_y, count_z), f32),
            pltpu.VMEM((block_y, grid_count, count_z), f32),
            pltpu.VMEM((count_x, count_z), f32),
            pltpu.VMEM((count_x, count_z), f32),
            pltpu.VMEM((orb_count, grid_count, planes, count_z), f32),
            pltpu.SemaphoreType.DMA((layers,)),
            pltpu.SemaphoreType.DMA((layers,)),
            pltpu.SemaphoreType.DMA,
            pltpu.SemaphoreType.DMA((2,)),
            pltpu.SemaphoreType.DMA((7,)),
            pltpu.SemaphoreType.DMA((7,)),
        ],
        compiler_params=pltpu.CompilerParams(
            collective_id=0, has_side_effects=True, vmem_limit_bytes=48 * 1024 * 1024
        ),
        name="step",
    )(occupations, orbitals, *tables)

    theta = TIME_STEP * (v_local + hartree)
    cosine = jnp.cos(theta)
    sine = jnp.sin(theta)
    real_part, imag_part = evolved[:, 0], evolved[:, 1]
    return jnp.stack(
        [real_part * cosine + imag_part * sine, imag_part * cosine - real_part * sine], 1
    )


def solution(mesh):
    return jax.shard_map(
        functools.partial(body, mesh.shape["grid"], mesh.shape["orb"]),
        mesh=mesh,
        in_specs=(
            P(("groups", "orb"), None, "grid", None, None),
            P(("groups", "grid"), None, None),
            P("groups"),
        ),
        out_specs=P(("groups", "orb"), None, "grid", None, None),
        check_vma=False,
    )
```

profile of v0, /device:TPU:513, one launch (start us, length us, event | category | flops | bytes accessed | tf_op | source)
XLA Modules:
  0.0 224.1 jit_solution(9616363723846225825)
XLA Ops:
  0.0 0.0 copy-start
  0.0 0.9 copy-done
  1.0 0.0 copy-start.1
  1.0 0.8 copy-done.1
  1.8 0.0 copy-start.2
  1.8 0.9 copy-done.2
  2.7 0.0 copy-start.3
  2.7 0.8 copy-done.3
  3.6 0.0 copy-start.4
  3.6 0.7 copy-done.4
  4.2 0.0 copy-start.5
  4.2 0.7 copy-done.5
  4.9 0.0 copy-start.6
  4.9 0.0 copy-start.7
  4.9 214.4 %step.1 = (f32[4,2,8,128,128]{4,3,2,1,0:T(8,128)S(1)}, f32[8,128,128]{2,1,0:T(8,128)S(1)}) custom-call(f32[32]{0:T(128)S(1)} %copy-done.4, f32[4,2,8,128,128]{4,3,2,1,0:T(8,128)} %psi_ref.1, f32[256,256]{1,0:T(8,128)S(1)} %copy-done, f32[256,256]{1,0:T(8,128)S(1)} %copy-done, f32[256,256]{1,0:T(8,128)S(1)} %copy-done.2, f32[128,128]{1,0:T(8,128)S(1)} %copy-done.1, ...), custom_call_target="tpu_custom_call" | custom-call | tf_op jit(solution)/shard_map/step/pallas_call | solution.py:326
  219.3 0.0 copy-done.6
  219.3 1.9 fusion.1
  221.2 0.0 copy-done.7
  221.2 0.9 multiply_add_fusion
  222.1 0.0 copy-start.8
  222.1 2.0 copy-done.8
  (1 shorter events, 0.0 us)
Async XLA Ops:
  0.0 0.9 copy-start
  1.0 0.8 copy-start.1
  1.8 0.9 copy-start.2
  2.7 0.8 copy-start.3
  3.6 0.7 copy-start.4
  4.2 0.7 copy-start.5
  4.9 214.4 %copy-start.6 = (f32[8,128,128]{2,1,0:T(8,128)S(1)}, f32[8,128,128]{2,1,0:T(8,128)}, u32[]{:S(2)}) copy-start(f32[8,128,128]{2,1,0:T(8,128)} %param.9) | copy-start | bytes 1572868
  4.9 216.3 %copy-start.7 = (f32[4,2,8,128,128]{4,3,2,1,0:T(8,128)S(1)}, f32[4,2,8,128,128]{4,3,2,1,0:T(8,128)}, u32[]{:S(2)}) copy-start(f32[4,2,8,128,128]{4,3,2,1,0:T(8,128)} %custom-call) | copy-start | bytes 12582916
  222.1 2.0 copy-start.8
where the time goes:
time: 224 us
  Pallas kernels  214 us (96%)
  local copies, waits for them, and re-layouts  6.9 us (3%)
  other arithmetic  2.82 us (1%)
    pallas_call x1, Pallas kernels, body(): pl.pallas_call(functools.partial(kernel, grid_count, orb_count), out_shap...  214 us
    unnamed x18, local copies, waits for them, and re-layouts  6.9 us

commit v1 on v0

v1 whole, which is shorter than its diff:
```python
import functools
import math

import jax
import jax.numpy as jnp
import numpy as np
from jax import lax
from jax.experimental import pallas as pl
from jax.experimental.pallas import tpu as pltpu
from jax.sharding import PartitionSpec as P

TIME_STEP = 0.05
KINETIC_RATE = 0.1
HARTREE_SCALE = math.pi
HIGHEST = lax.Precision.HIGHEST
MESH = pl.DeviceIdType.MESH


def wave_squared(length):
    mode_ids = np.arange(length)
    signed = np.where(mode_ids < (length + 1) // 2, mode_ids, mode_ids - length)
    return (2.0 * math.pi * signed / length) ** 2


def kinetic_table(length):
    phase = np.exp(-1j * KINETIC_RATE * wave_squared(length))
    circulant = np.fft.ifft(phase)
    ids = np.arange(length)
    full = circulant[(ids[:, None] - ids[None, :]) % length]
    return np.block([[full.real, -full.imag], [full.imag, full.real]]).astype(np.float32)


def hartley_table(length):
    ids = np.arange(length)
    angle = 2.0 * math.pi * (ids[:, None] * ids[None, :] % length) / length
    return ((np.cos(angle) + np.sin(angle)) / math.sqrt(length)).astype(np.float32)


def dot(left, right):
    return jnp.dot(left, right, precision=HIGHEST, preferred_element_type=jnp.float32)


def swap(block):
    return jnp.transpose(block, (1, 0, 2))


def kernel(
    grid_count,
    orb_count,
    table_slots,
    occ_hbm,
    psi_ref,
    v_hbm,
    *refs,
):
    n_tables = len(set(table_slots))
    tables_hbm = refs[:n_tables]
    out_ref = refs[n_tables]
    tables = refs[n_tables + 1 : 2 * n_tables + 1]
    (
    occ_ref,
    v_ref,
    own,
    lines_y,
    send_a,
    recv_a,
    lines_x,
    send_b,
    density,
    spectrum,
    parts,
    tiles,
    pencil,
    pencil_out,
    tiles_in,
    tiles_out,
    plane_in,
    plane,
    slabs,
    arrived,
    cosine,
    sine,
    table_sem,
    load_sem,
    recv_sem,
    recv_b_sem,
    send_sem,
    hart_send,
    hart_recv,
    ) = refs[2 * n_tables + 1 :]
    left_x, left_y, right_z, hart_x, hart_y, hart_z = [tables[i] for i in table_slots]
    g = lax.axis_index("grid")
    o = lax.axis_index("orb")
    layers, _, planes, count_y, count_z = own.shape
    count_x = planes * grid_count
    block_y = count_y // grid_count
    block_k = count_x // orb_count

    def load(l):
        return pltpu.make_async_copy(psi_ref.at[l], own.at[l], load_sem.at[l])

    def fetch(i):
        return pltpu.make_async_copy(tables_hbm[i], tables[i], table_sem.at[i])

    occ_copy = pltpu.make_async_copy(occ_hbm, occ_ref, table_sem.at[n_tables])
    v_copy = pltpu.make_async_copy(v_hbm, v_ref, table_sem.at[n_tables + 1])
    load(0).start()
    for i in range(n_tables):
        fetch(i).start()
    for l in range(1, layers):
        load(l).start()
    occ_copy.start()
    v_copy.start()

    barrier = pltpu.get_barrier_semaphore()

    def greet(axis, me, count):
        def one(off, carry):
            pl.semaphore_signal(
                barrier, inc=1, device_id={axis: lax.rem(me + off, count)}, device_id_type=MESH
            )
            return carry

        lax.fori_loop(1, count, one, 0)

    greet("grid", g, grid_count)
    greet("orb", o, orb_count)

    def send_all(axis, me, count, src, dst, s_sem, r_sem):
        def one(off, carry):
            to = lax.rem(me + off, count)
            pltpu.make_async_remote_copy(
                src_ref=src(to),
                dst_ref=dst,
                send_sem=s_sem,
                recv_sem=r_sem,
                device_id={axis: to},
                device_id_type=MESH,
            ).start()
            return carry

        lax.fori_loop(1, count, one, 0)

    def wait_for(ref, sem):
        pltpu.make_async_copy(ref, ref, sem).wait()

    def rows(start, size):
        return pl.ds(pl.multiple_of(start, 8), size)

    def along_y(l):
        load(l).wait()

        def pair(i, carry):
            both = [
                jnp.concatenate([own[l, 0, 2 * i + k], own[l, 1, 2 * i + k]], axis=0) for k in (0, 1)
            ]
            out = dot(left_y[...], jnp.concatenate(both, axis=1))
            lines_y[2 * i] = out[:, :count_z]
            lines_y[2 * i + 1] = out[:, count_z:]
            return carry

        lax.fori_loop(0, planes // 2, pair, 0)

    quads = 4 if grid_count % 4 == 0 else 1
    chunk_y = count_y // quads
    targets = grid_count // quads

    def along_z(l):
        def quad(i, carry):
            first = lax.rem(g // targets + i, quads) * targets
            start = first * block_y
            sides = []
            for c in (0, 1):
                block = lines_y[:, rows(c * count_y + start, chunk_y), :]
                sides.append(swap(block).reshape(chunk_y * planes, count_z))
            out = dot(jnp.concatenate(sides, axis=1), right_z[...])
            for c in (0, 1):
                part = out[:, c * count_z : (c + 1) * count_z]
                send_a[l, pl.ds(start, chunk_y), c] = part.reshape(chunk_y, planes, count_z)
            if l == 0:

                @pl.when(i == 0)
                def _():
                    pl.semaphore_wait(barrier, grid_count - 1 + orb_count - 1)

            return carry

        lax.fori_loop(0, quads, quad, 0)

    def forward(l):
        along_y(l)
        along_z(l)
        launch_forward(l)

    def launch_forward(l):
        def src(to):
            return send_a.at[l, pl.ds(to * block_y, block_y)]

        dst = recv_a.at[l, :, :, rows(g * planes, planes), :]
        pltpu.make_async_copy(src(g), dst, recv_sem.at[l]).start()
        send_all("grid", g, grid_count, src, dst, send_sem.at[0], recv_sem.at[l])

    def sum_modes(y):
        two = dot(hart_x[...], jnp.concatenate([density[y], density[y + 1]], axis=1))
        two = dot(jnp.concatenate([two[:, :count_z], two[:, count_z:]], axis=0), hart_z[...])
        spectrum[y] = two[:count_x]
        spectrum[y + 1] = two[count_x:]
        pair = pl.ds(y, 2)
        send_all(
            "orb",
            o,
            orb_count,
            lambda to: spectrum.at[pair, rows(to * block_k, block_k), :],
            parts.at[o, pair],
            hart_send.at[0],
            hart_recv.at[0],
        )

    def across_x(l):
        wait_for(recv_a.at[l], recv_sem.at[l])
        weight = occ_ref[o * layers + l]

        def pair(i, carry):
            both = [recv_a[l, 2 * i + k].reshape(2 * count_x, count_z) for k in (0, 1)]
            out = dot(left_x[...], jnp.concatenate(both, axis=1))
            for k in (0, 1):
                part = out[:, k * count_z : (k + 1) * count_z]
                lines_x[2 * i + k] = part
                squares = part[:count_x] * part[:count_x] + part[count_x:] * part[count_x:]
                if l == 0:
                    density[2 * i + k] = weight * squares
                else:
                    density[2 * i + k] += weight * squares
            if l == layers - 1:
                sum_modes(2 * i)
            return carry

        lax.fori_loop(0, block_y // 2, pair, 0)

        def turn(i, carry):
            for c in (0, 1):
                block = lines_x[:, rows(c * count_x + i * planes, planes), :]
                send_b[l, c, rows(i * planes, planes)] = swap(block)
            return carry

        lax.fori_loop(0, grid_count, turn, 0)

    def launch_back(l, c=None):
        part = (slice(None),) if c is None else (c,)

        def src(to):
            return send_b.at[(l, *part, pl.ds(to * planes, planes))]

        dst = arrived.at[(l, *part, slice(None), rows(g * block_y, block_y), slice(None))]
        pltpu.make_async_copy(src(g), dst, recv_b_sem.at[l]).start()
        send_all("grid", g, grid_count, src, dst, send_sem.at[1], recv_b_sem.at[l])

    for i in range(n_tables):
        fetch(i).wait()
    for l in range(layers):
        forward(l)
    occ_copy.wait()
    across_x(0)
    launch_back(0)
    for l in range(1, layers):
        across_x(l)

    wait_for(parts.at[pl.ds(0, orb_count - 1)], hart_recv.at[0])
    own_modes = rows(o * block_k, block_k)
    total = spectrum[:, own_modes, :]
    for off in range(1, orb_count):
        total += parts[lax.rem(o + off, orb_count)]
    tiles[...] = swap(total)

    send_all(
        "grid", g, grid_count, lambda to: tiles.at[to], pencil.at[rows(g * block_y, block_y)], hart_send.at[1], hart_recv.at[1]
    )
    pencil[rows(g * block_y, block_y)] = tiles[g]
    launch_back(1, 0)
    wait_for(pencil.at[pl.ds(0, count_y - block_y)], hart_recv.at[1])

    mode_x = o * block_k + g

    def square(mode, count):
        signed = jnp.where(mode < (count + 1) // 2, mode, mode - count).astype(jnp.float32)
        wave = signed * (2.0 * math.pi / count)
        return wave * wave

    mode_y = lax.broadcasted_iota(jnp.int32, (count_y, count_z), 0)
    mode_z = lax.broadcasted_iota(jnp.int32, (count_y, count_z), 1)
    waves = square(mode_x, count_x) + square(mode_y, count_y) + square(mode_z, count_z)
    anchor = waves <= 0.0
    scale = jnp.where(anchor, 0.0, HARTREE_SCALE / jnp.where(anchor, 1.0, waves))
    pencil_out[...] = dot(hart_y[...], dot(hart_y[...], pencil[...]) * scale)

    send_all(
        "grid", g, grid_count, lambda to: pencil_out.at[rows(to * block_y, block_y)], tiles_in.at[g], hart_send.at[2], hart_recv.at[2]
    )
    tiles_in[g] = pencil_out[rows(g * block_y, block_y)]
    launch_back(1, 1)
    launch_back(2)
    wait_for(tiles_in.at[pl.ds(0, grid_count - 1)], hart_recv.at[2])
    tiles_out[...] = swap(tiles_in[...])

    send_all(
        "orb", o, orb_count, lambda to: tiles_out.at[to], plane_in.at[rows(o * block_k, block_k)], hart_send.at[3], hart_recv.at[3]
    )
    plane_in[rows(o * block_k, block_k)] = tiles_out[o]
    wait_for(plane_in.at[pl.ds(0, count_x - block_k)], hart_recv.at[3])
    plane[...] = dot(dot(hart_x[...], plane_in[...]), hart_z[...])

    mine = slabs.at[o]
    send_all(
        "grid", g, grid_count, lambda to: plane.at[rows(to * planes, planes)], slabs.at[o, g], hart_send.at[4], hart_recv.at[4]
    )
    slabs[o, g] = plane[rows(g * planes, planes)]
    launch_back(3)
    wait_for(mine.at[pl.ds(0, grid_count - 1)], hart_recv.at[4])

    send_all("orb", o, orb_count, lambda to: slabs.at[o], slabs.at[o], hart_send.at[5], hart_recv.at[5])
    wait_for(slabs.at[pl.ds(0, orb_count - 1)], hart_recv.at[5])

    v_copy.wait()

    def spread(i, carry):
        part = rows(i * block_y, block_y)
        theta = TIME_STEP * (v_ref[:, part, :] + swap(slabs[:, i]))
        cosine[:, part, :] = jnp.cos(theta)
        sine[:, part, :] = jnp.sin(theta)
        return carry

    lax.fori_loop(0, grid_count, spread, 0)

    for l in range(layers):
        wait_for(arrived.at[l], recv_b_sem.at[l])

        def turn_phase(x, carry):
            real_part, imag_part = arrived[l, 0, x], arrived[l, 1, x]
            out_ref[l, 0, x] = real_part * cosine[x] + imag_part * sine[x]
            out_ref[l, 1, x] = imag_part * cosine[x] - real_part * sine[x]
            return carry

        lax.fori_loop(0, planes, turn_phase, 0)

    sent_a = send_a.at[:, pl.ds(0, count_y - block_y)]
    wait_for(sent_a, send_sem.at[0])
    sent_b = send_b.at[:, :, pl.ds(0, count_x - planes)]
    wait_for(sent_b, send_sem.at[1])
    wait_for(parts.at[pl.ds(0, orb_count - 1)], hart_send.at[0])
    wait_for(tiles.at[pl.ds(0, grid_count - 1)], hart_send.at[1])
    wait_for(pencil_out.at[pl.ds(0, count_y - block_y)], hart_send.at[2])
    wait_for(tiles_out.at[pl.ds(0, orb_count - 1)], hart_send.at[3])
    wait_for(plane.at[pl.ds(0, count_x - planes)], hart_send.at[4])
    wait_for(slabs.at[pl.ds(0, orb_count - 1)], hart_send.at[5])


def body(grid_count, orb_count, orbitals, v_local, occupations):
    layers, _, planes, count_y, count_z = orbitals.shape
    count_x = planes * grid_count
    block_y = count_y // grid_count
    block_k = count_x // orb_count
    assert block_y == orb_count and block_k == grid_count

    f32 = jnp.float32
    tables = (
        kinetic_table(count_x),
        kinetic_table(count_y),
        kinetic_table(count_z).T,
        hartley_table(count_x),
        hartley_table(count_y),
        hartley_table(count_z),
    )
    keys = [(t.shape, t.tobytes()) for t in tables]
    distinct = list(dict.fromkeys(keys))
    slots = tuple(distinct.index(key) for key in keys)
    tables = [jnp.asarray(tables[keys.index(key)]) for key in distinct]
    anyspace = pl.BlockSpec(memory_space=pltpu.HBM)
    return pl.pallas_call(
        functools.partial(kernel, grid_count, orb_count, slots),
        out_shape=pltpu.VMEM(orbitals.shape, f32),
        in_specs=[anyspace] * (3 + len(tables)),
        out_specs=pl.BlockSpec(memory_space=pltpu.VMEM),
        scratch_shapes=[pltpu.VMEM(t.shape, f32) for t in tables]
        + [
            pltpu.SMEM(occupations.shape, f32),
            pltpu.VMEM(v_local.shape, f32),
            pltpu.VMEM(orbitals.shape, f32),
            pltpu.VMEM((planes, 2 * count_y, count_z), f32),
            pltpu.VMEM((layers, count_y, 2, planes, count_z), f32),
            pltpu.VMEM((layers, block_y, 2, count_x, count_z), f32),
            pltpu.VMEM((block_y, 2 * count_x, count_z), f32),
            pltpu.VMEM((layers, 2, count_x, block_y, count_z), f32),
            pltpu.VMEM((block_y, count_x, count_z), f32),
            pltpu.VMEM((block_y, count_x, count_z), f32),
            pltpu.VMEM((orb_count, block_y, block_k, count_z), f32),
            pltpu.VMEM((grid_count, block_y, count_z), f32),
            pltpu.VMEM((count_y, count_z), f32),
            pltpu.VMEM((count_y, count_z), f32),
            pltpu.VMEM((grid_count, block_y, count_z), f32),
            pltpu.VMEM((block_y, grid_count, count_z), f32),
            pltpu.VMEM((count_x, count_z), f32),
            pltpu.VMEM((count_x, count_z), f32),
            pltpu.VMEM((orb_count, grid_count, planes, count_z), f32),
            pltpu.VMEM(orbitals.shape, f32),
            pltpu.VMEM(v_local.shape, f32),
            pltpu.VMEM(v_local.shape, f32),
            pltpu.SemaphoreType.DMA((len(tables) + 2,)),
            pltpu.SemaphoreType.DMA((layers,)),
            pltpu.SemaphoreType.DMA((layers,)),
            pltpu.SemaphoreType.DMA((layers,)),
            pltpu.SemaphoreType.DMA((2,)),
            pltpu.SemaphoreType.DMA((6,)),
            pltpu.SemaphoreType.DMA((6,)),
        ],
        compiler_params=pltpu.CompilerParams(
            collective_id=0, has_side_effects=True, vmem_limit_bytes=48 * 1024 * 1024
        ),
        name="step",
    )(*[pltpu.with_memory_space_constraint(a, pltpu.HBM) for a in (occupations, orbitals, v_local, *tables)])


def solution(mesh):
    return jax.shard_map(
        functools.partial(body, mesh.shape["grid"], mesh.shape["orb"]),
        mesh=mesh,
        in_specs=(
            P(("groups", "orb"), None, "grid", None, None),
            P(("groups", "grid"), None, None),
            P("groups"),
        ),
        out_specs=P(("groups", "orb"), None, "grid", None, None),
        check_vma=False,
    )
```

time: 224 us -> 213 us (0.951)
  local copies, waits for them, and re-layouts: 6.9 us -> 2.02 us
  Pallas kernels: 214 us -> 210 us
  other arithmetic: 2.82 us -> 0 us
    unnamed x18 -> x1, local copies, waits for them, and re-layouts: 6.9 us -> 2.02 us
    pallas_call x1, Pallas kernels: 214 us -> 210 us  [body(): pl.pallas_call(functools.partial(kernel, grid_count, orb_count, slots), o...]
where the time goes in v1:
time: 213 us; the launch traced here: 212 us
  Pallas kernels  210 us (99%)
    pallas_call x1, Pallas kernels, body(): pl.pallas_call(functools.partial(kernel, grid_count, orb_count, slots), o...  210 us

profile of v1, /device:TPU:513, one launch (start us, length us, event | category | flops | bytes accessed | tf_op | source)
XLA Modules:
  0.0 212.5 jit_solution(7486040873308572302)
XLA Ops:
  0.0 210.4 %step.1 = f32[4,2,8,128,128]{4,3,2,1,0:T(8,128)S(1)} custom-call(f32[32]{0:T(128)} %occ_hbm.1, f32[4,2,8,128,128]{4,3,2,1,0:T(8,128)} %psi_ref.1, f32[8,128,128]{2,1,0:T(8,128)} %v_hbm.1, f32[256,256]{1,0:T(8,128)} %constant.6.clone.refs_0_, f32[256,256]{1,0:T(8,128)} %constant.7.clone.refs_1_, f32[128,128]{1,0:T(8,128)} %constant.8.clone.refs_2_), custom_call_target="tpu_custom_call" | custom-call | tf_op jit(solution)/shard_map/step/pallas_call | solution.py:378
  210.5 2.0 copy.8

commit v2 on v1

--- a/solution.py
+++ b/solution.py
@@ -38,6 +38,29 @@
 
 def dot(left, right):
     return jnp.dot(left, right, precision=HIGHEST, preferred_element_type=jnp.float32)
+
+
+def split(value):
+    high = value.astype(jnp.bfloat16)
+    return high, (value - high.astype(jnp.float32)).astype(jnp.bfloat16)
+
+
+def dot_table_left(table, value):
+    high, low = split(value)
+    stacked = jnp.concatenate([high, high, low], axis=0)
+    return jnp.dot(table, stacked, preferred_element_type=jnp.float32)
+
+
+def dot_table_right(value, table):
+    high, low = split(value)
+    stacked = jnp.concatenate([high, high, low], axis=1)
+    return jnp.dot(stacked, table, preferred_element_type=jnp.float32)
+
+
+def three_parts(table, axis):
+    high = table.astype(jnp.bfloat16)
+    low = (table - high.astype(np.float32)).astype(jnp.bfloat16)
+    return np.concatenate([high, low, high], axis=axis)
 
 
 def swap(block):
@@ -127,8 +150,9 @@
     greet("orb", o, orb_count)
 
     def send_all(axis, me, count, src, dst, s_sem, r_sem):
-        def one(off, carry):
-            to = lax.rem(me + off, count)
+        def one(i, carry):
+            step = (i + 1) // 2
+            to = lax.rem(me + count // 2 + jnp.where(i % 2 == 1, count - step, step), count)
             pltpu.make_async_remote_copy(
                 src_ref=src(to),
                 dst_ref=dst,
@@ -139,7 +163,7 @@
             ).start()
             return carry
 
-        lax.fori_loop(1, count, one, 0)
+        lax.fori_loop(0, count - 1, one, 0)
 
     def wait_for(ref, sem):
         pltpu.make_async_copy(ref, ref, sem).wait()
@@ -154,51 +178,51 @@
             both = [
                 jnp.concatenate([own[l, 0, 2 * i + k], own[l, 1, 2 * i + k]], axis=0) for k in (0, 1)
             ]
-            out = dot(left_y[...], jnp.concatenate(both, axis=1))
+            out = dot_table_left(left_y[...], jnp.concatenate(both, axis=1))
             lines_y[2 * i] = out[:, :count_z]
             lines_y[2 * i + 1] = out[:, count_z:]
             return carry
 
         lax.fori_loop(0, planes // 2, pair, 0)
 
-    quads = 4 if grid_count % 4 == 0 else 1
-    chunk_y = count_y // quads
-    targets = grid_count // quads
+    half = grid_count // 2
+    quarters = [(0, half, half - 1, 1 - half), (half - 2, 2 - half, half - 3, 3 - half), (4, -4, 3, -3), (2, -2, 1, -1)]
+    if grid_count != 16:
+        quarters = [tuple(range(grid_count))]
 
     def along_z(l):
-        def quad(i, carry):
-            first = lax.rem(g // targets + i, quads) * targets
-            start = first * block_y
+        for n, offsets in enumerate(quarters):
+            targets = [lax.rem(g + off + grid_count, grid_count) for off in offsets]
             sides = []
             for c in (0, 1):
-                block = lines_y[:, rows(c * count_y + start, chunk_y), :]
-                sides.append(swap(block).reshape(chunk_y * planes, count_z))
-            out = dot(jnp.concatenate(sides, axis=1), right_z[...])
-            for c in (0, 1):
-                part = out[:, c * count_z : (c + 1) * count_z]
-                send_a[l, pl.ds(start, chunk_y), c] = part.reshape(chunk_y, planes, count_z)
-            if l == 0:
-
-                @pl.when(i == 0)
-                def _():
-                    pl.semaphore_wait(barrier, grid_count - 1 + orb_count - 1)
-
-            return carry
-
-        lax.fori_loop(0, quads, quad, 0)
+                blocks = [swap(lines_y[:, rows(c * count_y + to * block_y, block_y), :]) for to in targets]
+                sides.append(jnp.concatenate([b.reshape(block_y * planes, count_z) for b in blocks], axis=0))
+            out = dot_table_right(jnp.concatenate(sides, axis=1), right_z[...])
+            size = block_y * planes
+            for k, to in enumerate(targets):
+                for c in (0, 1):
+                    part = out[k * size : (k + 1) * size, c * count_z : (c + 1) * count_z]
+                    send_a[l, pl.ds(to * block_y, block_y), c] = part.reshape(block_y, planes, count_z)
+            if l == 0 and n == 0:
+                pl.semaphore_wait(barrier, grid_count - 1 + orb_count - 1)
+            dst = recv_a.at[l, :, :, rows(g * planes, planes), :]
+            for off, to in zip(offsets, targets):
+                src = send_a.at[l, pl.ds(to * block_y, block_y)]
+                if off == 0:
+                    pltpu.make_async_copy(src, dst, recv_sem.at[l]).start()
+                else:
+                    pltpu.make_async_remote_copy(
+                        src_ref=src,
+                        dst_ref=dst,
+                        send_sem=send_sem.at[0],
+                        recv_sem=recv_sem.at[l],
+                        device_id={"grid": to},
+                        device_id_type=MESH,
+                    ).start()
 
     def forward(l):
         along_y(l)
         along_z(l)
-        launch_forward(l)
-
-    def launch_forward(l):
-        def src(to):
-            return send_a.at[l, pl.ds(to * block_y, block_y)]
-
-        dst = recv_a.at[l, :, :, rows(g * planes, planes), :]
-        pltpu.make_async_copy(src(g), dst, recv_sem.at[l]).start()
-        send_all("grid", g, grid_count, src, dst, send_sem.at[0], recv_sem.at[l])
 
     def sum_modes(y):
         two = dot(hart_x[...], jnp.concatenate([density[y], density[y + 1]], axis=1))
@@ -222,7 +246,7 @@
 
         def pair(i, carry):
             both = [recv_a[l, 2 * i + k].reshape(2 * count_x, count_z) for k in (0, 1)]
-            out = dot(left_x[...], jnp.concatenate(both, axis=1))
+            out = dot_table_left(left_x[...], jnp.concatenate(both, axis=1))
             for k in (0, 1):
                 part = out[:, k * count_z : (k + 1) * count_z]
                 lines_x[2 * i + k] = part
@@ -298,7 +322,7 @@
     )
     tiles_in[g] = pencil_out[rows(g * block_y, block_y)]
     launch_back(1, 1)
-    launch_back(2)
+    launch_back(2, 0)
     wait_for(tiles_in.at[pl.ds(0, grid_count - 1)], hart_recv.at[2])
     tiles_out[...] = swap(tiles_in[...])
 
@@ -314,6 +338,7 @@
         "grid", g, grid_count, lambda to: plane.at[rows(to * planes, planes)], slabs.at[o, g], hart_send.at[4], hart_recv.at[4]
     )
     slabs[o, g] = plane[rows(g * planes, planes)]
+    launch_back(2, 1)
     launch_back(3)
     wait_for(mine.at[pl.ds(0, grid_count - 1)], hart_recv.at[4])
 
@@ -363,9 +388,9 @@
 
     f32 = jnp.float32
     tables = (
-        kinetic_table(count_x),
-        kinetic_table(count_y),
-        kinetic_table(count_z).T,
+        three_parts(kinetic_table(count_x), 1),
+        three_parts(kinetic_table(count_y), 1),
+        three_parts(kinetic_table(count_z).T, 0),
         hartley_table(count_x),
         hartley_table(count_y),
         hartley_table(count_z),
@@ -380,7 +405,7 @@
         out_shape=pltpu.VMEM(orbitals.shape, f32),
         in_specs=[anyspace] * (3 + len(tables)),
         out_specs=pl.BlockSpec(memory_space=pltpu.VMEM),
-        scratch_shapes=[pltpu.VMEM(t.shape, f32) for t in tables]
+        scratch_shapes=[pltpu.VMEM(t.shape, t.dtype) for t in tables]
         + [
             pltpu.SMEM(occupations.shape, f32),
             pltpu.VMEM(v_local.shape, f32),

time: 213 us -> 210 us (0.986)
    pallas_call x1, Pallas kernels: 210 us -> 208 us  [body(): pl.pallas_call(functools.partial(kernel, grid_count, orb_count, slots), o...]
where the time goes in v2:
time: 210 us
  Pallas kernels  208 us (99%)
    pallas_call x1, Pallas kernels, body(): pl.pallas_call(functools.partial(kernel, grid_count, orb_count, slots), o...  208 us

profile of v2, /device:TPU:513, one launch (start us, length us, event | category | flops | bytes accessed | tf_op | source)
XLA Modules:
  0.0 210.0 jit_solution(16279864453673967527)
XLA Ops:
  0.0 208.0 %step.1 = f32[4,2,8,128,128]{4,3,2,1,0:T(8,128)S(1)} custom-call(f32[32]{0:T(128)} %occ_hbm.1, f32[4,2,8,128,128]{4,3,2,1,0:T(8,128)} %psi_ref.1, f32[8,128,128]{2,1,0:T(8,128)} %v_hbm.1, bf16[256,768]{1,0:T(8,128)(2,1)} %constant.6.clone.refs_0_, bf16[768,256]{1,0:T(8,128)(2,1)} %constant.7.clone.refs_1_, f32[128,128]{1,0:T(8,128)} %constant.8.clone.refs_2_), custom_call_target="tpu_custom_call" | custom-call | tf_op jit(solution)/shard_map/step/pallas_call | solution.py:403
  208.0 2.0 copy.8

commit v3 on v2

--- a/solution.py
+++ b/solution.py
@@ -110,6 +110,7 @@
     send_sem,
     hart_send,
     hart_recv,
+    pair_sem,
     ) = refs[2 * n_tables + 1 :]
     left_x, left_y, right_z, hart_x, hart_y, hart_z = [tables[i] for i in table_slots]
     g = lax.axis_index("grid")
@@ -137,17 +138,23 @@
 
     barrier = pltpu.get_barrier_semaphore()
 
-    def greet(axis, me, count):
-        def one(off, carry):
-            pl.semaphore_signal(
-                barrier, inc=1, device_id={axis: lax.rem(me + off, count)}, device_id_type=MESH
-            )
-            return carry
-
-        lax.fori_loop(1, count, one, 0)
-
-    greet("grid", g, grid_count)
-    greet("orb", o, orb_count)
+    other = g + 1 - 2 * lax.rem(g, 2)
+
+    def greet(axis, me, count, stride):
+        def one(k, carry):
+            to = lax.rem(me + stride * k, count)
+            pl.semaphore_signal(barrier, inc=1, device_id={axis: to}, device_id_type=MESH)
+            return carry
+
+        lax.fori_loop(1, count // stride, one, 0)
+
+    greet("grid", g, grid_count, 2)
+    pl.semaphore_signal(barrier, inc=1, device_id={"grid": other}, device_id_type=MESH)
+    greet("orb", o, orb_count, 1)
+
+    def enter():
+        pl.semaphore_wait(barrier, grid_count // 2 + orb_count - 1)
+        pl.semaphore_signal(pair_sem, inc=1, device_id={"grid": other}, device_id_type=MESH)
 
     def send_all(axis, me, count, src, dst, s_sem, r_sem):
         def one(i, carry):
@@ -186,43 +193,69 @@
         lax.fori_loop(0, planes // 2, pair, 0)
 
     half = grid_count // 2
-    quarters = [(0, half, half - 1, 1 - half), (half - 2, 2 - half, half - 3, 3 - half), (4, -4, 3, -3), (2, -2, 1, -1)]
+    near = [(4, -4, 3, -3), (2, -2, 1, -1)]
+    full = [(0, half, half - 1, 1 - half), (half - 2, 2 - half, half - 3, 3 - half)] + near
+    evens = [(half, half - 2, 2 - half, 0), (4, -4, 2, -2)]
+    odds = [(half - 1, 1 - half, half - 3, 3 - half), (3, -3, 1, -1)]
     if grid_count != 16:
-        quarters = [tuple(range(grid_count))]
-
-    def along_z(l):
-        for n, offsets in enumerate(quarters):
-            targets = [lax.rem(g + off + grid_count, grid_count) for off in offsets]
-            sides = []
+        full = [tuple(range(grid_count))]
+        evens = [tuple(range(0, grid_count, 2))]
+        odds = [tuple(range(1, grid_count, 2))]
+
+    def target(off):
+        return lax.rem(g + off + grid_count, grid_count)
+
+    def along_z(l, offsets):
+        targets = [target(off) for off in offsets]
+        sides = []
+        for c in (0, 1):
+            blocks = [swap(lines_y[:, rows(c * count_y + to * block_y, block_y), :]) for to in targets]
+            sides.append(jnp.concatenate([b.reshape(block_y * planes, count_z) for b in blocks], axis=0))
+        out = dot_table_right(jnp.concatenate(sides, axis=1), right_z[...])
+        size = block_y * planes
+        for k, to in enumerate(targets):
             for c in (0, 1):
-                blocks = [swap(lines_y[:, rows(c * count_y + to * block_y, block_y), :]) for to in targets]
-                sides.append(jnp.concatenate([b.reshape(block_y * planes, count_z) for b in blocks], axis=0))
-            out = dot_table_right(jnp.concatenate(sides, axis=1), right_z[...])
-            size = block_y * planes
-            for k, to in enumerate(targets):
-                for c in (0, 1):
-                    part = out[k * size : (k + 1) * size, c * count_z : (c + 1) * count_z]
-                    send_a[l, pl.ds(to * block_y, block_y), c] = part.reshape(block_y, planes, count_z)
-            if l == 0 and n == 0:
-                pl.semaphore_wait(barrier, grid_count - 1 + orb_count - 1)
-            dst = recv_a.at[l, :, :, rows(g * planes, planes), :]
-            for off, to in zip(offsets, targets):
-                src = send_a.at[l, pl.ds(to * block_y, block_y)]
-                if off == 0:
-                    pltpu.make_async_copy(src, dst, recv_sem.at[l]).start()
-                else:
-                    pltpu.make_async_remote_copy(
-                        src_ref=src,
-                        dst_ref=dst,
-                        send_sem=send_sem.at[0],
-                        recv_sem=recv_sem.at[l],
-                        device_id={"grid": to},
-                        device_id_type=MESH,
-                    ).start()
+                part = out[k * size : (k + 1) * size, c * count_z : (c + 1) * count_z]
+                send_a[l, pl.ds(to * block_y, block_y), c] = part.reshape(block_y, planes, count_z)
+
+    def launch_forward(l, offsets):
+        dst = recv_a.at[l, :, :, rows(g * planes, planes), :]
+        for off in offsets:
+            to = target(off)
+            src = send_a.at[l, pl.ds(to * block_y, block_y)]
+            if off == 0:
+                pltpu.make_async_copy(src, dst, recv_sem.at[l]).start()
+            else:
+                pltpu.make_async_remote_copy(
+                    src_ref=src,
+                    dst_ref=dst,
+                    send_sem=send_sem.at[0],
+                    recv_sem=recv_sem.at[l],
+                    device_id={"grid": to},
+                    device_id_type=MESH,
+                ).start()
+
+    early = min(2, layers)
 
     def forward(l):
         along_y(l)
-        along_z(l)
+        if l >= early:
+            for offsets in full:
+                along_z(l, offsets)
+                launch_forward(l, offsets)
+            return
+        for offsets in evens:
+            along_z(l, offsets)
+            if l == 0 and offsets is evens[0]:
+                enter()
+            launch_forward(l, offsets)
+        for offsets in odds:
+            along_z(l, offsets)
+        if l == early - 1:
+            pl.semaphore_wait(pair_sem, 1)
+            for sent in range(early):
+                for offsets in odds:
+                    launch_forward(sent, offsets)
 
     def sum_modes(y):
         two = dot(hart_x[...], jnp.concatenate([density[y], density[y + 1]], axis=1))
@@ -436,6 +469,7 @@
             pltpu.SemaphoreType.DMA((2,)),
             pltpu.SemaphoreType.DMA((6,)),
             pltpu.SemaphoreType.DMA((6,)),
+            pltpu.SemaphoreType.REGULAR,
         ],
         compiler_params=pltpu.CompilerParams(
             collective_id=0, has_side_effects=True, vmem_limit_bytes=48 * 1024 * 1024

time: 210 us -> 204 us (0.971)
  Pallas kernels: 208 us -> 202 us
    pallas_call x1, Pallas kernels: 208 us -> 202 us  [body(): pl.pallas_call(functools.partial(kernel, grid_count, orb_count, slots), o...]
where the time goes in v3:
time: 204 us
  Pallas kernels  202 us (99%)
    pallas_call x1, Pallas kernels, body(): pl.pallas_call(functools.partial(kernel, grid_count, orb_count, slots), o...  202 us

profile of v3, /device:TPU:513, one launch (start us, length us, event | category | flops | bytes accessed | tf_op | source)
XLA Modules:
  0.0 204.3 jit_solution(2916607474830746916)
XLA Ops:
  0.0 202.3 %step.1 = f32[4,2,8,128,128]{4,3,2,1,0:T(8,128)S(1)} custom-call(f32[32]{0:T(128)} %occ_hbm.1, f32[4,2,8,128,128]{4,3,2,1,0:T(8,128)} %psi_ref.1, f32[8,128,128]{2,1,0:T(8,128)} %v_hbm.1, bf16[256,768]{1,0:T(8,128)(2,1)} %constant.6.clone.refs_0_, bf16[768,256]{1,0:T(8,128)(2,1)} %constant.7.clone.refs_1_, f32[128,128]{1,0:T(8,128)} %constant.8.clone.refs_2_), custom_call_target="tpu_custom_call" | custom-call | tf_op jit(solution)/shard_map/step/pallas_call | solution.py:436
  202.3 2.0 copy.8

commit v4 on v3

--- a/solution.py
+++ b/solution.py
@@ -235,7 +235,7 @@
                     device_id_type=MESH,
                 ).start()
 
-    early = min(2, layers)
+    early = min(3, layers)
 
     def forward(l):
         along_y(l)

time: 204 us -> 205 us (level)
  no operation moved by 1% of the time
where the time goes in v4:
time: 205 us
  Pallas kernels  203 us (99%)
    pallas_call x1, Pallas kernels, body(): pl.pallas_call(functools.partial(kernel, grid_count, orb_count, slots), o...  203 us

profile of v4, /device:TPU:513, one launch (start us, length us, event | category | flops | bytes accessed | tf_op | source)
XLA Modules:
  0.0 204.6 jit_solution(5352389604567280106)
XLA Ops:
  0.0 202.6 %step.1 = f32[4,2,8,128,128]{4,3,2,1,0:T(8,128)S(1)} custom-call(f32[32]{0:T(128)} %occ_hbm.1, f32[4,2,8,128,128]{4,3,2,1,0:T(8,128)} %psi_ref.1, f32[8,128,128]{2,1,0:T(8,128)} %v_hbm.1, bf16[256,768]{1,0:T(8,128)(2,1)} %constant.6.clone.refs_0_, bf16[768,256]{1,0:T(8,128)(2,1)} %constant.7.clone.refs_1_, f32[128,128]{1,0:T(8,128)} %constant.8.clone.refs_2_), custom_call_target="tpu_custom_call" | custom-call | tf_op jit(solution)/shard_map/step/pallas_call | solution.py:436
  202.6 2.0 copy.8
